TPU v7x, 32 devices: a whole 2x2x4 slice. The times are simulated.
32 devices in a mesh: groups: 2 (over y), row: 4 (over z), col: 4 (over x, core).
Axes of the slice: x: 2, y: 2, z: 4, core: 2. Of those that a mesh axis runs over, the one named last changes fastest.
Arguments:
- activations: bfloat16 [768, 4096], P(('groups', 'row'), 'col'), parts along dimension 0, may hold values from -52 to 52
- damping: float32 [8192], P(('groups', 'row')), parts along dimension 0, may hold values from 0.1 to 1
Outputs:
- factor: float32 [8192, 4096], P(('groups', 'row'), 'col'), parts along dimension 0
There are 2 independent parts, one for each index of `groups`. A program takes and returns all parts, laid end to end along the dimension named above; each array names one. Nothing has to cross between parts.
All inputs are finite; a program needn't handle non-finite values.
Results may differ from a plain program's by a relative error of at most 0.0003.
Values may be sent and summed in bfloat16 or wider, within the bound.
A program may use at most 64 MiB of HBM per device.

v0:
```python
import jax
import jax.numpy as jnp
from jax import lax
from jax.sharding import PartitionSpec as P

NB = 256
PANELS = 2


HIGHEST = lax.Precision.HIGHEST


def from_root(shard, axis, root):
    mine = lax.axis_index(axis) == root
    return lax.psum(jnp.where(mine, shard, jnp.zeros_like(shard)), axis)


def on_device(activations, damping):
    local_tokens = activations.shape[0]
    local_width = activations.shape[1]
    grid_size = lax.axis_size("row")
    row_dev = lax.axis_index("row")
    col_dev = lax.axis_index("col")
    columns = lax.all_gather(activations, "row", axis=0, tiled=True)
    mirrored = from_root(columns, "col", row_dev)
    gram_block = lax.dot_general(
        mirrored, columns, (((0,), (0,)), ((), ())), preferred_element_type=jnp.float32
    )
    diagonal_add = jnp.where(row_dev == col_dev, jnp.diag(damping), 0.0)
    matrix = gram_block / (local_tokens * grid_size) + diagonal_add
    local_index = jnp.arange(local_width, dtype=jnp.int32)
    global_rows = row_dev * local_width + local_index
    global_cols = col_dev * local_width + local_index

    def factor_step(panel_index, matrix):
        begin_at = panel_index * NB
        end_at = begin_at + NB
        owner_row = begin_at // local_width
        offset = begin_at - owner_row * local_width
        below = global_rows[:, None] >= end_at
        corner = lax.dynamic_slice(matrix, (offset, offset), (NB, NB))
        corner = lax.psum(jnp.where(row_dev == owner_row, corner, 0.0), "row")
        safe_corner = jnp.where(col_dev == owner_row, corner, jnp.eye(NB, dtype=jnp.float32))
        pivot_block = jnp.linalg.cholesky(safe_corner)
        own_block = lax.dynamic_slice_in_dim(matrix, offset, NB, 1)
        solved = jax.scipy.linalg.solve_triangular(pivot_block, own_block.T, lower=True).T
        row_side = lax.psum(jnp.where(col_dev == owner_row, solved, 0.0), "col")
        trail_rows = jnp.where(below, row_side, 0.0)
        trail_cols = lax.psum(jnp.where(row_dev == col_dev, trail_rows, 0.0), "row")
        trail_colsT = trail_cols.T
        update = jnp.dot(
            trail_rows, trail_colsT, precision=HIGHEST, preferred_element_type=jnp.float32
        )
        matrix = matrix - update
        placed = lax.dynamic_update_slice(trail_rows, pivot_block, (offset, 0))
        panel_rows = jnp.where(row_dev == owner_row, placed, trail_rows)
        written = lax.dynamic_update_slice(matrix, panel_rows, (0, offset))
        matrix = jnp.where(col_dev == owner_row, written, matrix)
        in_block = (global_rows[:, None] >= begin_at) & (global_rows[:, None] < end_at)
        right_side = global_cols[None, :] >= end_at
        return jnp.where(in_block & right_side, 0.0, matrix)

    return lax.fori_loop(0, PANELS, factor_step, matrix)


def solution(mesh):
    in_specs = (P(("groups", "row"), "col"), P(("groups", "row")))
    out_specs = P(("groups", "row"), "col")
    return jax.shard_map(
        on_device, mesh=mesh, in_specs=in_specs, out_specs=out_specs, check_vma=False
    )
```

profile of v0, /device:TPU:21, one launch (start us, length us, event | category | flops | bytes accessed | tf_op | source)
XLA Modules:
  0.0 490.0 jit_solution(14677081952462626796)
XLA Ops:
  6.5 16.0 %all_gather.3 = bf16[384,1024]{1,0:T(8,128)(2,1)S(1)} all-gather(bf16[96,1024]{1,0:T(8,128)(2,1)} %param.4), channel_id=1, replica_groups=mesh['groups'=2,'row'=4,'col'=4] {'row'}, dimensions={0}, use_global_device_ids=true | all-gather | bytes 983040 | tf_op jit(solution)/shard_map/all_gather | solution.py:24
  23.5 37.2 %all-reduce.6.cloned.1.call-done = bf16[384,1024]{1,0:T(8,128)(2,1)} async-done(((bf16[384,1024]{1,0:T(8,128)(2,1)}), bf16[384,1024]{1,0:T(8,128)(2,1)}) %all-reduce.6.cloned.1.call-update) | async-done | bytes 786448 | tf_op jit(solution)/shard_map/psum | solution.py:15
  60.7 4.4 select_add_fusion
  65.1 5.3 %copy.9 = f32[1024,1024]{0,1:T(8,128)} copy(f32[1024,1024]{1,0:T(8,128)} %select_add_fusion) | data formatting | bytes 8388608
  70.5 407.3 %while.20 = (s32[]{:T(128)}, f32[1024,1024]{0,1:T(8,128)}, s32[]{:T(128)}, s32[]{:T(128)}, pred[]{:T(512)}, /*index=5*/s32[]{:T(128)}, s32[]{:T(128)}, s32[]{:T(...) while((s32[]{:T(128)}, f32[1024,1024]{0,1:T(8,128)}, ...), condition=%wide.region_9.10_spmd.clone, body=%wide.region_1.9_spmd.clone.sunk | while | flops 3881984256 | bytes 53224180 | solution.py:63
  70.5 1.7 dynamic-slice_select_fusion.2
  73.6 34.5 %all-reduce.8.cloned.1.call-done = f32[256,256]{0,1:T(8,128)} async-done(((f32[256,256]{0,1:T(8,128)}), f32[256,256]{0,1:T(8,128)}) %all-reduce.8.cloned.1.call-update) | async-done | bytes 262160 | tf_op jit(solution)/shard_map/while/body/eval_jaxpr/psum | solution.py:42
  108.3 11.7 %cholesky.225 = f32[128,128]{1,0:T(8,128)S(1)} custom-call(f32[128,128]{1,0:T(8,128)S(1)} %cholesky.224), custom_call_target="Cholesky" | custom-call | tf_op jit(solution)/shard_map/while/body/eval_jaxpr/jit(cholesky)/cholesky | solution.py:44
  120.1 9.8 %custom-call.49 = f32[1,128,128]{1,2,0:T(8,128)S(1)} custom-call(f32[1,128,128]{2,1,0:T(8,128)S(1)} %get-tuple-element.322), custom_call_target="InvertDiagBlocksLowerTriangular" | custom-call | tf_op jit(solution)/shard_map/while/body/eval_jaxpr/jit(cholesky)/cholesky | solution.py:44
  130.4 11.7 %cholesky.227 = f32[128,128]{1,0:T(8,128)S(1)} custom-call(f32[128,128]{1,0:T(8,128)S(1)} %convolution_subtract_fusion.6), custom_call_target="Cholesky" | custom-call | tf_op jit(solution)/shard_map/while/body/eval_jaxpr/jit(cholesky)/cholesky | solution.py:44
  144.5 4.2 while.21
  145.1 1.4 dynamic-slice.21
  148.7 19.7 %custom-call.51 = f32[2,128,128]{1,2,0:T(8,128)S(1)} custom-call(f32[2,128,128]{2,1,0:T(8,128)S(1)} %get-tuple-element.326), custom_call_target="InvertDiagBlocksLowerTriangular" | custom-call | tf_op jit(solution)/shard_map/while/body/eval_jaxpr/jit(_solve_triangular)/triangular_solve | solution.py:46
  171.4 38.9 %all-reduce.10.cloned.1.call-done = f32[1024,256]{0,1:T(8,128)} async-done(((f32[1024,256]{0,1:T(8,128)}), f32[1024,256]{0,1:T(8,128)}) %all-reduce.10.cloned.1.call-update) | async-done | bytes 1048592 | tf_op jit(solution)/shard_map/while/body/eval_jaxpr/psum | solution.py:47
  210.4 2.5 broadcast_select_fusion.5
  212.9 51.9 %all-reduce.12.cloned.1.call-done = f32[1024,256]{0,1:T(8,128)} async-done(((f32[1024,256]{0,1:T(8,128)}), f32[1024,256]{0,1:T(8,128)}) %all-reduce.12.cloned.1.call-update) | async-done | bytes 1048592 | tf_op jit(solution)/shard_map/while/body/eval_jaxpr/psum | solution.py:49
  264.8 7.2 %convolution_subtract_fusion.8 = f32[1024,1024]{0,1:T(8,128)S(1)} fusion(f32[1024,1024]{0,1:T(8,128)} %get-tuple-element.370, f32[1024,256]{0,1:T(8,128)S(1)} %get-tuple-element.327, f32[1024,256]{0,1:T(8,128)} %all-reduce.12.cloned.1.call-done), kind=kOutput, calls=%fused_computation.5.clone.1 | convolution fusion | flops 3222274048 | bytes 10485760 | tf_op jit(solution)/shard_map/while/body/eval_jaxpr/dot_general | solution.py:51
  272.2 2.4 and_select_fusion.2
  274.6 1.7 dynamic-slice_select_fusion.2
  277.7 33.5 %all-reduce.8.cloned.1.call-done = f32[256,256]{0,1:T(8,128)} async-done(((f32[256,256]{0,1:T(8,128)}), f32[256,256]{0,1:T(8,128)}) %all-reduce.8.cloned.1.call-update) | async-done | bytes 262160 | tf_op jit(solution)/shard_map/while/body/eval_jaxpr/psum | solution.py:42
  311.5 11.7 %cholesky.225 = f32[128,128]{1,0:T(8,128)S(1)} custom-call(f32[128,128]{1,0:T(8,128)S(1)} %cholesky.224), custom_call_target="Cholesky" | custom-call | tf_op jit(solution)/shard_map/while/body/eval_jaxpr/jit(cholesky)/cholesky | solution.py:44
  323.2 9.8 %custom-call.49 = f32[1,128,128]{1,2,0:T(8,128)S(1)} custom-call(f32[1,128,128]{2,1,0:T(8,128)S(1)} %get-tuple-element.322), custom_call_target="InvertDiagBlocksLowerTriangular" | custom-call | tf_op jit(solution)/shard_map/while/body/eval_jaxpr/jit(cholesky)/cholesky | solution.py:44
  333.5 11.7 %cholesky.227 = f32[128,128]{1,0:T(8,128)S(1)} custom-call(f32[128,128]{1,0:T(8,128)S(1)} %convolution_subtract_fusion.6), custom_call_target="Cholesky" | custom-call | tf_op jit(solution)/shard_map/while/body/eval_jaxpr/jit(cholesky)/cholesky | solution.py:44
  347.7 4.2 while.21
  348.3 1.4 dynamic-slice.21
  351.9 19.7 %custom-call.51 = f32[2,128,128]{1,2,0:T(8,128)S(1)} custom-call(f32[2,128,128]{2,1,0:T(8,128)S(1)} %get-tuple-element.326), custom_call_target="InvertDiagBlocksLowerTriangular" | custom-call | tf_op jit(solution)/shard_map/while/body/eval_jaxpr/jit(_solve_triangular)/triangular_solve | solution.py:46
  374.6 38.9 %all-reduce.10.cloned.1.call-done = f32[1024,256]{0,1:T(8,128)} async-done(((f32[1024,256]{0,1:T(8,128)}), f32[1024,256]{0,1:T(8,128)}) %all-reduce.10.cloned.1.call-update) | async-done | bytes 1048592 | tf_op jit(solution)/shard_map/while/body/eval_jaxpr/psum | solution.py:47
  413.5 2.5 broadcast_select_fusion.5
  416.0 51.9 %all-reduce.12.cloned.1.call-done = f32[1024,256]{0,1:T(8,128)} async-done(((f32[1024,256]{0,1:T(8,128)}), f32[1024,256]{0,1:T(8,128)}) %all-reduce.12.cloned.1.call-update) | async-done | bytes 1048592 | tf_op jit(solution)/shard_map/while/body/eval_jaxpr/psum | solution.py:49
  467.9 7.2 %convolution_subtract_fusion.8 = f32[1024,1024]{0,1:T(8,128)S(1)} fusion(f32[1024,1024]{0,1:T(8,128)} %get-tuple-element.370, f32[1024,256]{0,1:T(8,128)S(1)} %get-tuple-element.327, f32[1024,256]{0,1:T(8,128)} %all-reduce.12.cloned.1.call-done), kind=kOutput, calls=%fused_computation.5.clone.1 | convolution fusion | flops 3222274048 | bytes 10485760 | tf_op jit(solution)/shard_map/while/body/eval_jaxpr/dot_general | solution.py:51
  475.4 2.4 and_select_fusion.2
  477.8 5.3 %copy.10 = f32[1024,1024]{1,0:T(8,128)} copy(f32[1024,1024]{0,1:T(8,128)} %get-tuple-element.167) | data formatting | bytes 8388608 | tf_op jit(solution)/shard_map/while | solution.py:63
  (89 shorter events, 19.4 us)
Async XLA Ops:
  6.5 54.2 %all-reduce.6.cloned.1.call-start = ((), (), s32[]{:S(2)}) async-start(), calls=%async_computation | async-start | bytes 1572864 | tf_op jit(solution)/shard_map/psum | solution.py:15
  70.5 37.6 %all-reduce.8.cloned.1.call-start = ((), (), s32[]{:S(2)}) async-start(), calls=%async_computation.1 | async-start | bytes 524288 | tf_op jit(solution)/shard_map/while/body/eval_jaxpr/psum | solution.py:42
  72.2 138.2 %all-reduce.10.cloned.1.call-start = ((), (), s32[]{:S(2)}) async-start(), calls=%async_computation.2 | async-start | bytes 2097152 | tf_op jit(solution)/shard_map/while/body/eval_jaxpr/psum | solution.py:47
  171.4 93.4 %all-reduce.12.cloned.1.call-start = ((), (), s32[]{:S(2)}) async-start(), calls=%async_computation.3 | async-start | bytes 2097152 | tf_op jit(solution)/shard_map/while/body/eval_jaxpr/psum | solution.py:49
  274.6 36.6 %all-reduce.8.cloned.1.call-start = ((), (), s32[]{:S(2)}) async-start(), calls=%async_computation.1 | async-start | bytes 524288 | tf_op jit(solution)/shard_map/while/body/eval_jaxpr/psum | solution.py:42
  276.3 137.2 %all-reduce.10.cloned.1.call-start = ((), (), s32[]{:S(2)}) async-start(), calls=%async_computation.2 | async-start | bytes 2097152 | tf_op jit(solution)/shard_map/while/body/eval_jaxpr/psum | solution.py:47
  374.5 93.4 %all-reduce.12.cloned.1.call-start = ((), (), s32[]{:S(2)}) async-start(), calls=%async_computation.3 | async-start | bytes 2097152 | tf_op jit(solution)/shard_map/while/body/eval_jaxpr/psum | solution.py:49
Sparse Core Ops, SparseCore 0:
  23.6 37.0 all-reduce.5
  73.6 34.4 all-reduce.7
  171.5 38.8 all-reduce.9
  213.0 51.7 all-reduce.11
  277.4 33.7 all-reduce.7
  374.6 38.8 all-reduce.9
  416.1 51.7 all-reduce.11
where the time goes:
time: 494 us; the launch traced here: 490 us
  waiting for transfers between devices  287 us (58%)
  other arithmetic  124 us (25%)
  matrix products  23.5 us (5%)
  local copies, waits for them, and re-layouts  22.5 us (5%)
  blocking collectives  16 us (3%)
  between operations  13.4 us (3%)
    psum x2, waiting for transfers between devices, factor_step(): trail_cols = lax.psum(jnp.where(row_dev == col_dev, trail_rows, 0.0), 'row')  104 us
    psum x2, waiting for transfers between devices, factor_step(): row_side = lax.psum(jnp.where(col_dev == owner_row, solved, 0.0), 'col')  77.9 us
    psum x2, waiting for transfers between devices, factor_step(): corner = lax.psum(jnp.where(row_dev == owner_row, corner, 0.0), 'row')  68.1 us
    another operation x12, other arithmetic, factor_step(): pivot_block = jnp.linalg.cholesky(safe_corner)  67.9 us
    another operation x6, other arithmetic, factor_step(): jax.scipy.linalg.solve_triangular(pivot_block, own_block.T, lower=True)  39.4 us
    psum x1, waiting for transfers between devices, from_root(): return lax.psum(jnp.where(mine, shard, jnp.zeros_like(shard)), axis)  37.2 us
    all_gather x1, blocking collectives, on_device(): columns = lax.all_gather(activations, 'row', axis=0, tiled=True)  16 us
    dot_general x2, matrix products, factor_step(): jnp.dot(trail_rows, trail_colsT, precision=HIGHEST, preferred_element_typ...  14.3 us
  transfers between devices with their start and end apart: 7, of which 7 were waited for; matrix products, arithmetic and copies ran while one was open for 1% of the time, Pallas kernels for 0%

commit v1 on v0

v1 whole, which is shorter than its diff:
```python
import functools

import jax
import jax.numpy as jnp
from jax import lax
from jax.experimental import pallas as pl
from jax.experimental.pallas import tpu as pltpu
from jax.sharding import PartitionSpec as P

NB = 256
PANELS = 2
LEAD = NB * PANELS
BLK = 128
SUB = 8
HIGHEST = lax.Precision.HIGHEST
MESH = pl.DeviceIdType.MESH


def dot(a, b, dims, precision=None):
    return lax.dot_general(
        a, b, (dims, ((), ())), precision=precision, preferred_element_type=jnp.float32
    )


def split2(x):
    hi = x.astype(jnp.bfloat16)
    lo = (x - hi.astype(jnp.float32)).astype(jnp.bfloat16)
    return hi, lo


def factor_block(s):
    lane = lax.broadcasted_iota(jnp.int32, (SUB, BLK), 1)
    sub = lax.broadcasted_iota(jnp.int32, (SUB, BLK), 0)
    groups = BLK // SUB
    rows = [s[SUB * g : SUB * (g + 1), :] for g in range(groups)]
    upper, inverse = [], []
    for g in range(groups):
        mine = rows[g]
        first = SUB * g
        cols = [
            jnp.broadcast_to(mine[:, first + k : first + k + 1], (SUB, BLK)) for k in range(SUB)
        ]
        diag = jnp.zeros((SUB, BLK), jnp.float32)
        recip = jnp.zeros((SUB, BLK), jnp.float32)
        for j in range(SUB):
            pivot = jnp.broadcast_to(cols[j][j : j + 1, :], (SUB, BLK))
            inv = 1.0 / pivot
            below = sub > j
            at = lane == first + j
            w = jnp.where(below, cols[j] * inv, 0.0)
            diag = jnp.where(sub == j, pivot, diag)
            recip = jnp.where(sub == j, inv, recip)
            for k in range(j + 1, SUB):
                cols[k] = cols[k] - w * jnp.broadcast_to(cols[k][j : j + 1, :], (SUB, BLK))
            row = jnp.where(at, 1.0, jnp.broadcast_to(mine[j : j + 1, :], (SUB, BLK)))
            mine = jnp.where(at & below, 0.0, mine) - w * row
        on = lane == sub + first
        low = lane < sub + first
        inv_part = jnp.where(low, mine, jnp.where(on, 1.0, 0.0))
        root = 1.0 / jnp.sqrt(diag)
        upper.append(jnp.where(low, 0.0, mine) * root)
        inverse.append(inv_part * root)
        if g < groups - 1:
            spread = jnp.where(lane >= first + SUB, mine, inv_part)
            inside = (lane >= first) & (lane < first + SUB)
            weights = (mine * recip).T
            for h in range(g + 1, groups):
                block = weights[SUB * h : SUB * (h + 1), :]
                acc = jnp.where(inside, 0.0, rows[h])
                for j in range(SUB):
                    acc = acc - jnp.broadcast_to(block[:, j : j + 1], (SUB, BLK)) * jnp.broadcast_to(
                        spread[j : j + 1, :], (SUB, BLK)
                    )
                rows[h] = acc
    return jnp.concatenate(upper, 0), jnp.concatenate(inverse, 0)


def gather_kernel(
    nr, nc, a_ref, damp_ref, cols_ref, mir_ref, b_ref, w_ref, l_ref, lead, dlead,
    z_send, z_recv, d_send, d_recv, f_send, f_recv, m_send, m_recv,
):
    local, width = a_ref.shape
    tokens = local * nr
    lw = min(width, LEAD)
    leads = LEAD // lw
    r = lax.axis_index("row")
    c = lax.axis_index("col")
    rest = width - lw

    def rows_of(i):
        return pl.ds(pl.multiple_of(i * local, 16), local)

    barrier = pltpu.get_barrier_semaphore()
    for d in range(1, nr):
        pl.semaphore_signal(
            barrier, inc=1, device_id={"row": lax.rem(r + d, nr)}, device_id_type=MESH
        )
    for d in range(1, nc):
        pl.semaphore_signal(
            barrier, inc=1, device_id={"col": lax.rem(c + d, nc)}, device_id_type=MESH
        )
    pl.semaphore_wait(barrier, nr + nc - 2)

    def z_copy(part, src_row, d):
        span = pl.ds(0, lw) if part == 0 else pl.ds(lw, rest)
        return pltpu.make_async_remote_copy(
            src_ref=a_ref.at[:, span],
            dst_ref=cols_ref.at[rows_of(src_row), span],
            send_sem=z_send.at[part, d],
            recv_sem=z_recv.at[part, src_row],
            device_id={"row": lax.rem(r + d, nr)},
            device_id_type=MESH,
        )

    def d_copy(src_row, d):
        span = pl.ds(pl.multiple_of(src_row * lw, 128), lw)
        return pltpu.make_async_remote_copy(
            src_ref=damp_ref.at[:, pl.ds(0, lw)],
            dst_ref=dlead.at[:, span],
            send_sem=d_send.at[d],
            recv_sem=d_recv.at[src_row],
            device_id={"row": lax.rem(r + d, nr)},
            device_id_type=MESH,
        )

    def f_copy(src_row, src_col, d):
        place = lead.at[rows_of(src_row), pl.ds(pl.multiple_of(src_col * lw, 128), lw)]
        return pltpu.make_async_remote_copy(
            src_ref=cols_ref.at[rows_of(src_row), pl.ds(0, lw)],
            dst_ref=place,
            send_sem=f_send.at[src_row, d],
            recv_sem=f_recv.at[src_col, src_row],
            device_id={"col": lax.rem(c + d, nc)},
            device_id_type=MESH,
        )

    def m_copy(src_row, d):
        return pltpu.make_async_remote_copy(
            src_ref=cols_ref.at[rows_of(src_row), :],
            dst_ref=mir_ref.at[rows_of(src_row), :],
            send_sem=m_send.at[src_row, d],
            recv_sem=m_recv.at[src_row],
            device_id={"col": lax.rem(c + d, nc)},
            device_id_type=MESH,
        )

    parts = 2 if rest else 1
    for d in range(1, nr):
        z_copy(0, r, d).start()

    @pl.when(r < leads)
    def _():
        for d in range(1, nr):
            d_copy(r, d).start()
        dlead[:, pl.ds(pl.multiple_of(jnp.minimum(r, leads - 1) * lw, 128), lw)] = damp_ref[:, :lw]

    cols_ref[rows_of(r), :] = a_ref[...]
    if rest:
        for d in range(1, nr):
            z_copy(1, r, d).start()

    for e in range(1, nr):
        z_copy(0, lax.rem(r + e, nr), e).wait_recv()

        @pl.when(c < leads)
        def _():
            for d in range(1, nc):
                f_copy(lax.rem(r + e, nr), c, d).start()

    @pl.when(c < leads)
    def _():
        for d in range(1, nc):
            f_copy(r, c, d).start()
        lead[:, pl.ds(pl.multiple_of(jnp.minimum(c, leads - 1) * lw, 128), lw)] = cols_ref[:, :lw]

    for src_col in range(leads):

        @pl.when(c != src_col)
        def _():
            for i in range(nr):
                f_copy(i, src_col, 1).wait_recv()

    for src_row in range(leads):

        @pl.when(r != src_row)
        def _():
            d_copy(src_row, 1).wait_recv()

    eye_t = lax.broadcasted_iota(jnp.int32, (tokens, tokens), 0) == lax.broadcasted_iota(
        jnp.int32, (tokens, tokens), 1
    )
    w_ref[...] = jnp.where(eye_t, 1.0 / tokens, 0.0)

    def step(k, carry):
        span = pl.ds(pl.multiple_of(k * BLK, BLK), BLK)
        a_k = lead[:, span].astype(jnp.float32)
        z = dot(w_ref[...], a_k, ((1,), (0,)), HIGHEST)
        eye = lax.broadcasted_iota(jnp.int32, (BLK, BLK), 0) == lax.broadcasted_iota(
            jnp.int32, (BLK, BLK), 1
        )
        s = dot(a_k, z, ((0,), (0,)), HIGHEST) + jnp.where(eye, dlead[:, span], 0.0)
        upper, inverse = factor_block(s)
        l_ref[span, :] = upper.T
        b = dot(inverse, z, ((1,), (1,)), HIGHEST)
        b_ref[span, :] = b
        w_ref[...] = w_ref[...] - dot(b, b, ((0,), (0,)), HIGHEST)
        return carry

    step(0, 0)

    if rest:
        for e in range(1, nr):
            z_copy(1, lax.rem(r + e, nr), e).wait_recv()

    @pl.when(r == c)
    def _():
        for i in range(nr):
            for d in range(1, nc):
                m_copy(i, d).start()
        mir_ref[...] = cols_ref[...]

    lax.fori_loop(1, LEAD // BLK, step, 0)

    @pl.when(r != c)
    def _():
        for i in range(nr):
            m_copy(i, 1).wait_recv()

    @pl.when(r == c)
    def _():
        for i in range(nr):
            for d in range(1, nc):
                m_copy(i, d).wait_send()

    @pl.when(c < leads)
    def _():
        for i in range(nr):
            for d in range(1, nc):
                f_copy(i, c, d).wait_send()

    @pl.when(r < leads)
    def _():
        for d in range(1, nr):
            d_copy(r, d).wait_send()

    for part in range(parts):
        for d in range(1, nr):
            z_copy(part, r, d).wait_send()


def update_kernel(cols_ref, mir_ref, b_ref, w_ref, l_ref, damp_ref, out_ref, y_hi, y_lo):
    tile, width = out_ref.shape
    i = pl.program_id(0)
    r = lax.axis_index("row")
    c = lax.axis_index("col")
    lw = min(width, LEAD)

    @pl.when(i == 0)
    def _():
        hi, lo = split2(w_ref[...])
        y = dot(hi, cols_ref[...], ((1,), (0,))) + dot(lo, cols_ref[...], ((1,), (0,)))
        y_hi[...], y_lo[...] = split2(y)

    a = mir_ref[...]
    s = dot(a, y_hi[...], ((0,), (0,))) + dot(a, y_lo[...], ((0,), (0,)))
    row = i * tile + lax.broadcasted_iota(jnp.int32, (tile, width), 0)
    col = lax.broadcasted_iota(jnp.int32, (tile, width), 1)
    s = s + jnp.where((row == col) & (r == c), damp_ref[...], 0.0)
    out_ref[...] = jnp.where(r * width + row >= LEAD, s, 0.0)

    @pl.when(c * width < LEAD)
    def _():
        base = pl.multiple_of(jnp.minimum(c * width, LEAD - lw), BLK)
        hi, lo = split2(b_ref[pl.ds(base, lw), :])
        p = dot(a, hi, ((0,), (1,))) + dot(a, lo, ((0,), (1,)))
        grow = r * width + i * tile + lax.broadcasted_iota(jnp.int32, (tile, lw), 0)
        gcol = c * width + lax.broadcasted_iota(jnp.int32, (tile, lw), 1)
        out_ref[:, :lw] = jnp.where(grow >= gcol, p, 0.0)
        for t in range(tile // BLK):
            for q in range(lw // BLK):

                @pl.when((r == c) & (i * (tile // BLK) + t == q))
                def _():
                    out_ref[t * BLK : (t + 1) * BLK, q * BLK : (q + 1) * BLK] = l_ref[
                        pl.ds(base + q * BLK, BLK), :
                    ]


def on_device(nr, nc, activations, damping):
    local, width = activations.shape
    tokens = local * nr
    lw = min(width, LEAD)
    leads = LEAD // lw
    damp = damping.reshape(1, width)
    vmem = pl.BlockSpec(memory_space=pltpu.VMEM)
    dma = pltpu.SemaphoreType.DMA
    cols, mir, b, w, l = pl.pallas_call(
        functools.partial(gather_kernel, nr, nc),
        out_shape=(
            jax.ShapeDtypeStruct((tokens, width), jnp.bfloat16),
            jax.ShapeDtypeStruct((tokens, width), jnp.bfloat16),
            jax.ShapeDtypeStruct((LEAD, tokens), jnp.float32),
            jax.ShapeDtypeStruct((tokens, tokens), jnp.float32),
            jax.ShapeDtypeStruct((LEAD, BLK), jnp.float32),
        ),
        in_specs=[vmem] * 2,
        out_specs=(vmem,) * 5,
        scratch_shapes=[
            pltpu.VMEM((tokens, LEAD), jnp.bfloat16),
            pltpu.VMEM((1, LEAD), jnp.float32),
            dma((2, nr)),
            dma((2, nr)),
            dma((nr,)),
            dma((leads,)),
            dma((nr, nc)),
            dma((leads, nr)),
            dma((nr, nc)),
            dma((nr,)),
        ],
        compiler_params=pltpu.CompilerParams(
            collective_id=0, has_side_effects=True, vmem_limit_bytes=60 * 2**20
        ),
        name="gather_factor",
    )(activations, damp)
    tile = min(256, width)
    whole = lambda shape: pl.BlockSpec(shape, lambda i: (0, 0))
    return pl.pallas_call(
        update_kernel,
        grid=(width // tile,),
        out_shape=jax.ShapeDtypeStruct((width, width), jnp.float32),
        in_specs=[
            whole((tokens, width)),
            pl.BlockSpec((tokens, tile), lambda i: (0, i)),
            whole((LEAD, tokens)),
            whole((tokens, tokens)),
            whole((LEAD, BLK)),
            whole((1, width)),
        ],
        out_specs=pl.BlockSpec((tile, width), lambda i: (i, 0)),
        scratch_shapes=[
            pltpu.VMEM((tokens, width), jnp.bfloat16),
            pltpu.VMEM((tokens, width), jnp.bfloat16),
        ],
        compiler_params=pltpu.CompilerParams(vmem_limit_bytes=60 * 2**20),
        name="update",
    )(cols, mir, b, w, l, damp)


def solution(mesh):
    in_specs = (P(("groups", "row"), "col"), P(("groups", "row")))
    out_specs = P(("groups", "row"), "col")
    body = functools.partial(on_device, mesh.shape["row"], mesh.shape["col"])
    return jax.shard_map(
        body, mesh=mesh, in_specs=in_specs, out_specs=out_specs, check_vma=False
    )
```

time: 494 us -> 69.8 us (0.14)
  the two profiles are of different devices: /device:TPU:21 before, /device:TPU:11 now
where the time goes in v1:
time: 69.8 us; the launch traced here: 69.6 us
  Pallas kernels  69.6 us (100%)
    pallas_call x1, Pallas kernels, on_device(): pl.pallas_call(functools.partial(gather_kernel, nr, nc), out_shape=(jax.S...  62.2 us
    pallas_call x1, Pallas kernels, on_device(): pl.pallas_call(update_kernel, grid=(width // tile,), out_shape=jax.ShapeD...  7.43 us

profile of v1, /device:TPU:11, one launch (start us, length us, event | category | flops | bytes accessed | tf_op | source)
XLA Modules:
  0.0 69.6 jit_solution(4276180237905848612)
XLA Ops:
  0.0 62.2 %gather_factor.1 = (bf16[384,1024]{1,0:T(8,128)(2,1)}, bf16[384,1024]{1,0:T(8,128)(2,1)}, f32[512,384]{1,0:T(8,128)}, f32[384,384]{1,0:T(8,128)}, f32[512,128]{1,0:T(8,128)}) custom-call(bf16[96,1024]{1,0:T(8,128)(2,1)} %a_ref.1, f32[1,1024]{1,0:T(1,128)} %bitcast.1), custom_call_target="tpu_custom_call" | custom-call | tf_op jit(solution)/shard_map/gather_factor/pallas_call | solution.py:297
  62.2 7.4 %update.1 = f32[1024,1024]{1,0:T(8,128)} custom-call(bf16[384,1024]{1,0:T(8,128)(2,1)} %get-tuple-element.10.cols_ref, bf16[384,1024]{1,0:T(8,128)(2,1)} %get-tuple-element.11.mir_ref, f32[512,384]{1,0:T(8,128)} %get-tuple-element.12.b_ref, f32[384,384]{1,0:T(8,128)} %get-tuple-element.13.w_ref, f32[512,128]{1,0:T(8,128)} %get-tuple-element.14.l_ref, ...), custom_call_target="tpu_custom_call" | custom-call | tf_op jit(solution)/shard_map/update/pallas_call | solution.py:327

commit v2 on v1

--- a/solution.py
+++ b/solution.py
@@ -28,56 +28,104 @@
     return hi, lo
 
 
-def factor_block(s):
+def split3(x):
+    hi = x.astype(jnp.bfloat16)
+    rest = x - hi.astype(jnp.float32)
+    mid = rest.astype(jnp.bfloat16)
+    lo = (rest - mid.astype(jnp.float32)).astype(jnp.bfloat16)
+    return hi, mid, lo
+
+
+def dot_pair(x, y, dims):
+    (xh, xl), (yh, yl) = x, y
+    return dot(xh, yl, dims) + dot(xl, yh, dims) + dot(xh, yh, dims)
+
+
+def eliminate(s):
     lane = lax.broadcasted_iota(jnp.int32, (SUB, BLK), 1)
     sub = lax.broadcasted_iota(jnp.int32, (SUB, BLK), 0)
     groups = BLK // SUB
+
+    def lanes(x, k):
+        return jnp.broadcast_to(x[:, k : k + 1], (SUB, BLK))
+
+    def subs(x, k):
+        return jnp.broadcast_to(x[k : k + 1, :], (SUB, BLK))
+
     rows = [s[SUB * g : SUB * (g + 1), :] for g in range(groups)]
     upper, inverse = [], []
     for g in range(groups):
         mine = rows[g]
         first = SUB * g
-        cols = [
-            jnp.broadcast_to(mine[:, first + k : first + k + 1], (SUB, BLK)) for k in range(SUB)
-        ]
+        inside = (lane >= first) & (lane < first + SUB)
+        more = g + 1 < groups
+        cols = [lanes(mine, first + k) for k in range(SUB)]
+        if more:
+            after = [lanes(rows[g + 1], first + k) for k in range(SUB)]
+            follow = jnp.where(inside, 0.0, rows[g + 1])
         diag = jnp.zeros((SUB, BLK), jnp.float32)
         recip = jnp.zeros((SUB, BLK), jnp.float32)
         for j in range(SUB):
-            pivot = jnp.broadcast_to(cols[j][j : j + 1, :], (SUB, BLK))
+            pivot = subs(cols[j], j)
             inv = 1.0 / pivot
             below = sub > j
             at = lane == first + j
-            w = jnp.where(below, cols[j] * inv, 0.0)
+            w = jnp.where(below, cols[j], 0.0) * inv
             diag = jnp.where(sub == j, pivot, diag)
             recip = jnp.where(sub == j, inv, recip)
+            row = jnp.where(at, 1.0, subs(mine, j))
+            row = jnp.where(inside & (lane > first + j), 0.0, row)
+            if more:
+                v = after[j] * inv
             for k in range(j + 1, SUB):
-                cols[k] = cols[k] - w * jnp.broadcast_to(cols[k][j : j + 1, :], (SUB, BLK))
-            row = jnp.where(at, 1.0, jnp.broadcast_to(mine[j : j + 1, :], (SUB, BLK)))
-            mine = jnp.where(at & below, 0.0, mine) - w * row
+                head = subs(cols[k], j)
+                cols[k] = cols[k] - w * head
+                if more:
+                    after[k] = after[k] - v * head
+            full = jnp.where(at, 1.0, subs(mine, j))
+            mine = jnp.where(at & below, 0.0, mine) - w * full
+            if more:
+                follow = follow - v * row
         on = lane == sub + first
         low = lane < sub + first
         inv_part = jnp.where(low, mine, jnp.where(on, 1.0, 0.0))
-        root = 1.0 / jnp.sqrt(diag)
+        root = lax.rsqrt(diag)
+        root = root * (1.5 - 0.5 * diag * root * root)
         upper.append(jnp.where(low, 0.0, mine) * root)
         inverse.append(inv_part * root)
-        if g < groups - 1:
+        if more:
+            rows[g + 1] = follow
+        if g + 2 < groups:
             spread = jnp.where(lane >= first + SUB, mine, inv_part)
-            inside = (lane >= first) & (lane < first + SUB)
             weights = (mine * recip).T
-            for h in range(g + 1, groups):
+            for h in range(g + 2, groups):
                 block = weights[SUB * h : SUB * (h + 1), :]
                 acc = jnp.where(inside, 0.0, rows[h])
                 for j in range(SUB):
-                    acc = acc - jnp.broadcast_to(block[:, j : j + 1], (SUB, BLK)) * jnp.broadcast_to(
-                        spread[j : j + 1, :], (SUB, BLK)
-                    )
+                    acc = acc - jnp.broadcast_to(block[:, j : j + 1], (SUB, BLK)) * subs(spread, j)
                 rows[h] = acc
     return jnp.concatenate(upper, 0), jnp.concatenate(inverse, 0)
 
 
+def factor_step(a_k, damp, w):
+    eye = lax.broadcasted_iota(jnp.int32, (BLK, BLK), 0) == lax.broadcasted_iota(
+        jnp.int32, (BLK, BLK), 1
+    )
+    over = ((1,), (0,))
+    wh, wm, wl = split3(w)
+    z = dot(wl, a_k, over) + dot(wm, a_k, over) + dot(wh, a_k, over)
+    zh, zm, zl = split3(z)
+    first = ((0,), (0,))
+    s = dot(a_k, zl, first) + dot(a_k, zm, first) + dot(a_k, zh, first)
+    upper, inverse = eliminate(s + jnp.where(eye, damp, 0.0))
+    b = dot_pair(split2(inverse), (zh, zm), ((1,), (1,)))
+    bs = split2(b)
+    return upper.T, b, w - dot_pair(bs, bs, first)
+
+
 def gather_kernel(
     nr, nc, a_ref, damp_ref, cols_ref, mir_ref, b_ref, w_ref, l_ref, lead, dlead,
-    z_send, z_recv, d_send, d_recv, f_send, f_recv, m_send, m_recv,
+    z_send, z_recv, d_send, d_recv, f_send, f_recv, fp_send, m_send, m_recv, mp_send,
 ):
     local, width = a_ref.shape
     tokens = local * nr
@@ -86,6 +134,12 @@
     r = lax.axis_index("row")
     c = lax.axis_index("col")
     rest = width - lw
+    chips = nc // 2
+    chip = c // 2
+    core = lax.rem(c, 2)
+    partner = c + 1 - 2 * core
+    lead_chips = (leads + 1) // 2
+    halves = nr // 2
 
     def rows_of(i):
         return pl.ds(pl.multiple_of(i * local, 16), local)
@@ -123,14 +177,30 @@
             device_id_type=MESH,
         )
 
+    def target(i, d):
+        there = 2 * lax.rem(chip + d, chips) + lax.rem(i, 2)
+        return {"col": partner if d == 0 else there}
+
+    def place(src_row, src_col):
+        return lead.at[rows_of(src_row), pl.ds(pl.multiple_of(src_col * lw, 128), lw)]
+
     def f_copy(src_row, src_col, d):
-        place = lead.at[rows_of(src_row), pl.ds(pl.multiple_of(src_col * lw, 128), lw)]
         return pltpu.make_async_remote_copy(
             src_ref=cols_ref.at[rows_of(src_row), pl.ds(0, lw)],
-            dst_ref=place,
+            dst_ref=place(src_row, src_col),
             send_sem=f_send.at[src_row, d],
             recv_sem=f_recv.at[src_col, src_row],
-            device_id={"col": lax.rem(c + d, nc)},
+            device_id=target(src_row, d),
+            device_id_type=MESH,
+        )
+
+    def fp_copy(src_row, src_col):
+        return pltpu.make_async_remote_copy(
+            src_ref=place(src_row, src_col),
+            dst_ref=place(src_row, src_col),
+            send_sem=fp_send.at[src_col, src_row],
+            recv_sem=f_recv.at[src_col, src_row],
+            device_id={"col": partner},
             device_id_type=MESH,
         )
 
@@ -140,13 +210,33 @@
             dst_ref=mir_ref.at[rows_of(src_row), :],
             send_sem=m_send.at[src_row, d],
             recv_sem=m_recv.at[src_row],
-            device_id={"col": lax.rem(c + d, nc)},
-            device_id_type=MESH,
-        )
-
-    parts = 2 if rest else 1
-    for d in range(1, nr):
-        z_copy(0, r, d).start()
+            device_id=target(src_row, d),
+            device_id_type=MESH,
+        )
+
+    def mp_copy(src_row):
+        return pltpu.make_async_remote_copy(
+            src_ref=mir_ref.at[rows_of(src_row), :],
+            dst_ref=mir_ref.at[rows_of(src_row), :],
+            send_sem=mp_send.at[src_row],
+            recv_sem=m_recv.at[src_row],
+            device_id={"col": partner},
+            device_id_type=MESH,
+        )
+
+    def others():
+        for part in range(2 if rest else 1):
+            for d in range(1, nr):
+                z_copy(part, r, d).start()
+
+    @pl.when(c < leads)
+    def _():
+        for d in range(1, nr):
+            z_copy(0, r, d).start()
+
+    @pl.when(chip >= lead_chips)
+    def _():
+        others()
 
     @pl.when(r < leads)
     def _():
@@ -155,30 +245,50 @@
         dlead[:, pl.ds(pl.multiple_of(jnp.minimum(r, leads - 1) * lw, 128), lw)] = damp_ref[:, :lw]
 
     cols_ref[rows_of(r), :] = a_ref[...]
-    if rest:
-        for d in range(1, nr):
-            z_copy(1, r, d).start()
-
-    for e in range(1, nr):
-        z_copy(0, lax.rem(r + e, nr), e).wait_recv()
-
-        @pl.when(c < leads)
-        def _():
-            for d in range(1, nc):
-                f_copy(lax.rem(r + e, nr), c, d).start()
 
     @pl.when(c < leads)
     def _():
-        for d in range(1, nc):
+        for e in range(1, nr):
+            i = lax.rem(r + e, nr)
+            z_copy(0, i, e).wait_recv()
+            for d in list(range(1, chips)) + [0]:
+                f_copy(i, c, d).start()
+        for d in list(range(1, chips)) + [0]:
             f_copy(r, c, d).start()
+        if rest:
+            for d in range(1, nr):
+                z_copy(1, r, d).start()
         lead[:, pl.ds(pl.multiple_of(jnp.minimum(c, leads - 1) * lw, 128), lw)] = cols_ref[:, :lw]
 
+    if lead_chips * 2 > leads:
+
+        @pl.when((c >= leads) & (chip < lead_chips))
+        def _():
+            f_copy(lax.rem(r + 1, nr), 0, 0).wait_recv()
+            others()
+
     for src_col in range(leads):
 
-        @pl.when(c != src_col)
-        def _():
-            for i in range(nr):
-                f_copy(i, src_col, 1).wait_recv()
+        @pl.when((c != src_col) & (chip == src_col // 2))
+        def _():
+            for e in range(nr):
+                i = lax.rem(r + e, nr)
+                if src_col == 0 and e == 1:
+
+                    @pl.when(c < leads)
+                    def _():
+                        f_copy(i, src_col, 0).wait_recv()
+
+                else:
+                    f_copy(i, src_col, 0).wait_recv()
+
+        @pl.when(chip != src_col // 2)
+        def _():
+            for q in range(halves):
+                f_copy(2 * q + core, src_col, 0).wait_recv()
+                fp_copy(2 * q + core, src_col).start()
+            for q in range(halves):
+                f_copy(2 * q + 1 - core, src_col, 0).wait_recv()
 
     for src_row in range(leads):
 
@@ -191,51 +301,69 @@
     )
     w_ref[...] = jnp.where(eye_t, 1.0 / tokens, 0.0)
 
-    def step(k, carry):
+    @pl.loop(0, LEAD // BLK)
+    def _(k):
         span = pl.ds(pl.multiple_of(k * BLK, BLK), BLK)
-        a_k = lead[:, span].astype(jnp.float32)
-        z = dot(w_ref[...], a_k, ((1,), (0,)), HIGHEST)
-        eye = lax.broadcasted_iota(jnp.int32, (BLK, BLK), 0) == lax.broadcasted_iota(
-            jnp.int32, (BLK, BLK), 1
-        )
-        s = dot(a_k, z, ((0,), (0,)), HIGHEST) + jnp.where(eye, dlead[:, span], 0.0)
-        upper, inverse = factor_block(s)
-        l_ref[span, :] = upper.T
-        b = dot(inverse, z, ((1,), (1,)), HIGHEST)
+        l, b, w = factor_step(lead[:, span], dlead[:, span], w_ref[...])
+        l_ref[span, :] = l
         b_ref[span, :] = b
-        w_ref[...] = w_ref[...] - dot(b, b, ((0,), (0,)), HIGHEST)
-        return carry
-
-    step(0, 0)
-
-    if rest:
-        for e in range(1, nr):
-            z_copy(1, lax.rem(r + e, nr), e).wait_recv()
+        w_ref[...] = w
+
+        @pl.when(k == 1)
+        def _():
+            @pl.when(c < leads)
+            def _():
+                if rest:
+                    for e in range(1, nr):
+                        z_copy(1, lax.rem(r + e, nr), e).wait_recv()
+
+            @pl.when(c >= leads)
+            def _():
+                for part in range(2 if rest else 1):
+                    for e in range(1, nr):
+                        z_copy(part, lax.rem(r + e, nr), e).wait_recv()
+
+            @pl.when(r == c)
+            def _():
+                for i in range(nr):
+                    for d in list(range(1, chips)) + [0]:
+                        m_copy(i, d).start()
+                mir_ref[...] = cols_ref[...]
+
+        @pl.when((k == 2) & (chip != r // 2))
+        def _():
+            for q in range(halves):
+                m_copy(2 * q + core, 0).wait_recv()
+                mp_copy(2 * q + core).start()
+
+    @pl.when((r != c) & (chip == r // 2))
+    def _():
+        for i in range(nr):
+            m_copy(i, 0).wait_recv()
+
+    @pl.when(chip != r // 2)
+    def _():
+        for q in range(halves):
+            m_copy(2 * q + 1 - core, 0).wait_recv()
+            mp_copy(2 * q + core).wait_send()
 
     @pl.when(r == c)
     def _():
         for i in range(nr):
-            for d in range(1, nc):
-                m_copy(i, d).start()
-        mir_ref[...] = cols_ref[...]
-
-    lax.fori_loop(1, LEAD // BLK, step, 0)
-
-    @pl.when(r != c)
+            for d in range(chips):
+                m_copy(i, d).wait_send()
+
+    for src_col in range(leads):
+
+        @pl.when(chip != src_col // 2)
+        def _():
+            for q in range(halves):
+                fp_copy(2 * q + core, src_col).wait_send()
+
+    @pl.when(c < leads)
     def _():
         for i in range(nr):
-            m_copy(i, 1).wait_recv()
-
-    @pl.when(r == c)
-    def _():
-        for i in range(nr):
-            for d in range(1, nc):
-                m_copy(i, d).wait_send()
-
-    @pl.when(c < leads)
-    def _():
-        for i in range(nr):
-            for d in range(1, nc):
+            for d in range(chips):
                 f_copy(i, c, d).wait_send()
 
     @pl.when(r < leads)
@@ -243,7 +371,7 @@
         for d in range(1, nr):
             d_copy(r, d).wait_send()
 
-    for part in range(parts):
+    for part in range(2 if rest else 1):
         for d in range(1, nr):
             z_copy(part, r, d).wait_send()
 
@@ -261,7 +389,7 @@
         y = dot(hi, cols_ref[...], ((1,), (0,))) + dot(lo, cols_ref[...], ((1,), (0,)))
         y_hi[...], y_lo[...] = split2(y)
 
-    a = mir_ref[...]
+    a = mir_ref[:, pl.ds(pl.multiple_of(i * tile, BLK), tile)]
     s = dot(a, y_hi[...], ((0,), (0,))) + dot(a, y_lo[...], ((0,), (0,)))
     row = i * tile + lax.broadcasted_iota(jnp.int32, (tile, width), 0)
     col = lax.broadcasted_iota(jnp.int32, (tile, width), 1)
@@ -292,6 +420,7 @@
     lw = min(width, LEAD)
     leads = LEAD // lw
     damp = damping.reshape(1, width)
+    limit = min(60 * 2**20, 16 * 2**20 + 48 * tokens * tokens)
     vmem = pl.BlockSpec(memory_space=pltpu.VMEM)
     dma = pltpu.SemaphoreType.DMA
     cols, mir, b, w, l = pl.pallas_call(
@@ -312,36 +441,30 @@
             dma((2, nr)),
             dma((nr,)),
             dma((leads,)),
-            dma((nr, nc)),
+            dma((nr, nc // 2)),
             dma((leads, nr)),
-            dma((nr, nc)),
+            dma((leads, nr)),
+            dma((nr, nc // 2)),
+            dma((nr,)),
             dma((nr,)),
         ],
         compiler_params=pltpu.CompilerParams(
-            collective_id=0, has_side_effects=True, vmem_limit_bytes=60 * 2**20
+            collective_id=0, has_side_effects=True, vmem_limit_bytes=limit
         ),
         name="gather_factor",
     )(activations, damp)
     tile = min(256, width)
-    whole = lambda shape: pl.BlockSpec(shape, lambda i: (0, 0))
     return pl.pallas_call(
         update_kernel,
         grid=(width // tile,),
         out_shape=jax.ShapeDtypeStruct((width, width), jnp.float32),
-        in_specs=[
-            whole((tokens, width)),
-            pl.BlockSpec((tokens, tile), lambda i: (0, i)),
-            whole((LEAD, tokens)),
-            whole((tokens, tokens)),
-            whole((LEAD, BLK)),
-            whole((1, width)),
-        ],
+        in_specs=[vmem] * 6,
         out_specs=pl.BlockSpec((tile, width), lambda i: (i, 0)),
         scratch_shapes=[
             pltpu.VMEM((tokens, width), jnp.bfloat16),
             pltpu.VMEM((tokens, width), jnp.bfloat16),
         ],
-        compiler_params=pltpu.CompilerParams(vmem_limit_bytes=60 * 2**20),
+        compiler_params=pltpu.CompilerParams(vmem_limit_bytes=limit),
         name="update",
     )(cols, mir, b, w, l, damp)
 

time: 69.8 us -> 54.8 us (0.79)
  the two profiles are of different devices: /device:TPU:11 before, /device:TPU:21 now
where the time goes in v2:
time: 54.8 us; the launch traced here: 54.6 us
  Pallas kernels  53 us (97%)
  local copies, waits for them, and re-layouts  1.61 us (3%)
    pallas_call x1, Pallas kernels, on_device(): pl.pallas_call(functools.partial(gather_kernel, nr, nc), out_shape=(jax.S...  47.6 us
    pallas_call x1, Pallas kernels, on_device(): pl.pallas_call(update_kernel, grid=(width // tile,), out_shape=jax.ShapeD...  5.33 us
    unnamed x4, local copies, waits for them, and re-layouts  1.61 us

profile of v2, /device:TPU:21, one launch (start us, length us, event | category | flops | bytes accessed | tf_op | source)
XLA Modules:
  0.0 54.6 jit_solution(16819993285493510313)
XLA Ops:
  0.0 0.0 copy-start
  0.0 0.9 %copy-done = bf16[96,1024]{1,0:T(8,128)(2,1)S(1)} copy-done((bf16[96,1024]{1,0:T(8,128)(2,1)S(1)}, bf16[96,1024]{1,0:T(8,128)(2,1)}, u32[]{:S(2)}) %copy-start) | copy-done | bytes 196632
  0.9 0.0 copy-start.1
  0.9 0.7 %copy-done.1 = f32[1024]{0:T(1024)S(1)} copy-done((f32[1024]{0:T(1024)S(1)}, f32[1024]{0:T(1024)}, u32[]{:S(2)}) %copy-start.1) | copy-done | bytes 4120
  1.6 47.6 %gather_factor.1 = (bf16[384,1024]{1,0:T(8,128)(2,1)S(1)}, bf16[384,1024]{1,0:T(8,128)(2,1)S(1)}, f32[512,384]{1,0:T(8,128)S(1)}, f32[384,384]{1,0:T(8,128)S(1)}, f32[512,128]{1,0:T(8,128)S(1)}) custom-call(bf16[96,1024]{1,0:T(8,128)(2,1)S(1)} %copy-done, f32[1,1024]{1,0:T(1,128)S(1)} %bitcast.1), custom_call_target="tpu_custom_call" | custom-call | tf_op jit(solution)/shard_map/gather_factor/pallas_call | solution.py:426
  49.3 5.3 %update.1 = f32[1024,1024]{1,0:T(8,128)} custom-call(bf16[384,1024]{1,0:T(8,128)(2,1)S(1)} %get-tuple-element.10.cols_ref, bf16[384,1024]{1,0:T(8,128)(2,1)S(1)} %get-tuple-element.11.mir_ref, f32[512,384]{1,0:T(8,128)S(1)} %get-tuple-element.12.b_ref, f32[384,384]{1,0:T(8,128)S(1)} %get-tuple-element.13.w_ref, f32[512,128]{1,0:T(8,128)S(1)} %get-tuple-element.14.l_ref, ...), custom_call_target="tpu_custom_call" | custom-call | tf_op jit(solution)/shard_map/update/pallas_call | solution.py:457
Async XLA Ops:
  0.0 0.9 %copy-start = (bf16[96,1024]{1,0:T(8,128)(2,1)S(1)}, bf16[96,1024]{1,0:T(8,128)(2,1)}, u32[]{:S(2)}) copy-start(bf16[96,1024]{1,0:T(8,128)(2,1)} %a_ref.1) | copy-start | bytes 589828
  0.9 0.7 %copy-start.1 = (f32[1024]{0:T(1024)S(1)}, f32[1024]{0:T(1024)}, u32[]{:S(2)}) copy-start(f32[1024]{0:T(1024)} %param.3) | copy-start | bytes 12292

commit v3 on v2

--- a/solution.py
+++ b/solution.py
@@ -118,16 +118,17 @@
     first = ((0,), (0,))
     s = dot(a_k, zl, first) + dot(a_k, zm, first) + dot(a_k, zh, first)
     upper, inverse = eliminate(s + jnp.where(eye, damp, 0.0))
-    b = dot_pair(split2(inverse), (zh, zm), ((1,), (1,)))
-    bs = split2(b)
-    return upper.T, b, w - dot_pair(bs, bs, first)
+    last = ((1,), (1,))
+    bt = dot_pair((zh, zm), split2(inverse), last)
+    bs = split2(bt)
+    return upper.T, bt, w - dot_pair(bs, bs, last)
 
 
 def gather_kernel(
-    nr, nc, a_ref, damp_ref, cols_ref, mir_ref, b_ref, w_ref, l_ref, lead, dlead,
+    nr, nc, a_hbm, damp_hbm, cols_ref, mir_ref, b_ref, w_ref, l_ref, lead, dlead, damp_ref, load,
     z_send, z_recv, d_send, d_recv, f_send, f_recv, fp_send, m_send, m_recv, mp_send,
 ):
-    local, width = a_ref.shape
+    local, width = a_hbm.shape
     tokens = local * nr
     lw = min(width, LEAD)
     leads = LEAD // lw
@@ -140,10 +141,15 @@
     partner = c + 1 - 2 * core
     lead_chips = (leads + 1) // 2
     halves = nr // 2
+    every = [0, 1] if rest else [0]
 
     def rows_of(i):
         return pl.ds(pl.multiple_of(i * local, 16), local)
 
+    bring = pltpu.make_async_copy(a_hbm, cols_ref.at[rows_of(r), :], load.at[0])
+    bring_damp = pltpu.make_async_copy(damp_hbm, damp_ref, load.at[1])
+    bring.start()
+    bring_damp.start()
     barrier = pltpu.get_barrier_semaphore()
     for d in range(1, nr):
         pl.semaphore_signal(
@@ -154,11 +160,13 @@
             barrier, inc=1, device_id={"col": lax.rem(c + d, nc)}, device_id_type=MESH
         )
     pl.semaphore_wait(barrier, nr + nc - 2)
+    bring.wait()
+    bring_damp.wait()
 
     def z_copy(part, src_row, d):
         span = pl.ds(0, lw) if part == 0 else pl.ds(lw, rest)
         return pltpu.make_async_remote_copy(
-            src_ref=a_ref.at[:, span],
+            src_ref=cols_ref.at[rows_of(r), span],
             dst_ref=cols_ref.at[rows_of(src_row), span],
             send_sem=z_send.at[part, d],
             recv_sem=z_recv.at[part, src_row],
@@ -224,10 +232,14 @@
             device_id_type=MESH,
         )
 
-    def others():
-        for part in range(2 if rest else 1):
-            for d in range(1, nr):
-                z_copy(part, r, d).start()
+    def others(parts):
+        for part in parts:
+            for d in range(nr):
+                ahead = lax.rem(c + d - r + nr, nr)
+
+                @pl.when(ahead != 0)
+                def _():
+                    z_copy(part, r, ahead).start()
 
     @pl.when(c < leads)
     def _():
@@ -236,15 +248,13 @@
 
     @pl.when(chip >= lead_chips)
     def _():
-        others()
+        others(every)
 
     @pl.when(r < leads)
     def _():
         for d in range(1, nr):
             d_copy(r, d).start()
         dlead[:, pl.ds(pl.multiple_of(jnp.minimum(r, leads - 1) * lw, 128), lw)] = damp_ref[:, :lw]
-
-    cols_ref[rows_of(r), :] = a_ref[...]
 
     @pl.when(c < leads)
     def _():
@@ -256,8 +266,7 @@
         for d in list(range(1, chips)) + [0]:
             f_copy(r, c, d).start()
         if rest:
-            for d in range(1, nr):
-                z_copy(1, r, d).start()
+            others([1])
         lead[:, pl.ds(pl.multiple_of(jnp.minimum(c, leads - 1) * lw, 128), lw)] = cols_ref[:, :lw]
 
     if lead_chips * 2 > leads:
@@ -265,7 +274,7 @@
         @pl.when((c >= leads) & (chip < lead_chips))
         def _():
             f_copy(lax.rem(r + 1, nr), 0, 0).wait_recv()
-            others()
+            others(every)
 
     for src_col in range(leads):
 
@@ -296,6 +305,19 @@
         def _():
             d_copy(src_row, 1).wait_recv()
 
+    def z_wait():
+        @pl.when(c < leads)
+        def _():
+            if rest:
+                for e in range(1, nr):
+                    z_copy(1, lax.rem(r + e, nr), e).wait_recv()
+
+        @pl.when(c >= leads)
+        def _():
+            for part in every:
+                for e in range(1, nr):
+                    z_copy(part, lax.rem(r + e, nr), e).wait_recv()
+
     eye_t = lax.broadcasted_iota(jnp.int32, (tokens, tokens), 0) == lax.broadcasted_iota(
         jnp.int32, (tokens, tokens), 1
     )
@@ -306,35 +328,26 @@
         span = pl.ds(pl.multiple_of(k * BLK, BLK), BLK)
         l, b, w = factor_step(lead[:, span], dlead[:, span], w_ref[...])
         l_ref[span, :] = l
-        b_ref[span, :] = b
+        b_ref[:, span] = b
         w_ref[...] = w
 
-        @pl.when(k == 1)
-        def _():
-            @pl.when(c < leads)
-            def _():
-                if rest:
-                    for e in range(1, nr):
-                        z_copy(1, lax.rem(r + e, nr), e).wait_recv()
-
-            @pl.when(c >= leads)
-            def _():
-                for part in range(2 if rest else 1):
-                    for e in range(1, nr):
-                        z_copy(part, lax.rem(r + e, nr), e).wait_recv()
-
-            @pl.when(r == c)
-            def _():
-                for i in range(nr):
-                    for d in list(range(1, chips)) + [0]:
-                        m_copy(i, d).start()
-                mir_ref[...] = cols_ref[...]
+        @pl.when((k == 0) & (r == c))
+        def _():
+            z_wait()
+            for i in range(nr):
+                for d in list(range(1, chips)) + [0]:
+                    m_copy(i, d).start()
+            mir_ref[...] = cols_ref[...]
 
         @pl.when((k == 2) & (chip != r // 2))
         def _():
             for q in range(halves):
                 m_copy(2 * q + core, 0).wait_recv()
                 mp_copy(2 * q + core).start()
+
+    @pl.when(r != c)
+    def _():
+        z_wait()
 
     @pl.when((r != c) & (chip == r // 2))
     def _():
@@ -383,27 +396,38 @@
     c = lax.axis_index("col")
     lw = min(width, LEAD)
 
-    @pl.when(i == 0)
-    def _():
+    base = pl.multiple_of(jnp.minimum(c * width, LEAD - lw), BLK)
+
+    def fill(span):
         hi, lo = split2(w_ref[...])
-        y = dot(hi, cols_ref[...], ((1,), (0,))) + dot(lo, cols_ref[...], ((1,), (0,)))
-        y_hi[...], y_lo[...] = split2(y)
+        a_c = cols_ref[:, span]
+        y = dot(hi, a_c, ((1,), (0,))) + dot(lo, a_c, ((1,), (0,)))
+        y_hi[:, span], y_lo[:, span] = split2(y)
+
+    @pl.when((i == 0) & (c * width < LEAD))
+    def _():
+        y_hi[:, :lw], y_lo[:, :lw] = split2(b_ref[:, pl.ds(base, lw)])
+
+    @pl.when((i == 0) & (c * width >= LEAD))
+    def _():
+        fill(slice(0, lw))
+
+    if width > lw:
+
+        @pl.when(i == 0)
+        def _():
+            fill(slice(lw, width))
 
     a = mir_ref[:, pl.ds(pl.multiple_of(i * tile, BLK), tile)]
     s = dot(a, y_hi[...], ((0,), (0,))) + dot(a, y_lo[...], ((0,), (0,)))
     row = i * tile + lax.broadcasted_iota(jnp.int32, (tile, width), 0)
     col = lax.broadcasted_iota(jnp.int32, (tile, width), 1)
     s = s + jnp.where((row == col) & (r == c), damp_ref[...], 0.0)
-    out_ref[...] = jnp.where(r * width + row >= LEAD, s, 0.0)
+    keep = r * width + row >= jnp.minimum(c * width + col, LEAD)
+    out_ref[...] = jnp.where(keep, s, 0.0)
 
     @pl.when(c * width < LEAD)
     def _():
-        base = pl.multiple_of(jnp.minimum(c * width, LEAD - lw), BLK)
-        hi, lo = split2(b_ref[pl.ds(base, lw), :])
-        p = dot(a, hi, ((0,), (1,))) + dot(a, lo, ((0,), (1,)))
-        grow = r * width + i * tile + lax.broadcasted_iota(jnp.int32, (tile, lw), 0)
-        gcol = c * width + lax.broadcasted_iota(jnp.int32, (tile, lw), 1)
-        out_ref[:, :lw] = jnp.where(grow >= gcol, p, 0.0)
         for t in range(tile // BLK):
             for q in range(lw // BLK):
 
@@ -428,15 +452,17 @@
         out_shape=(
             jax.ShapeDtypeStruct((tokens, width), jnp.bfloat16),
             jax.ShapeDtypeStruct((tokens, width), jnp.bfloat16),
-            jax.ShapeDtypeStruct((LEAD, tokens), jnp.float32),
+            jax.ShapeDtypeStruct((tokens, LEAD), jnp.float32),
             jax.ShapeDtypeStruct((tokens, tokens), jnp.float32),
             jax.ShapeDtypeStruct((LEAD, BLK), jnp.float32),
         ),
-        in_specs=[vmem] * 2,
+        in_specs=[pl.BlockSpec(memory_space=pltpu.HBM)] * 2,
         out_specs=(vmem,) * 5,
         scratch_shapes=[
             pltpu.VMEM((tokens, LEAD), jnp.bfloat16),
             pltpu.VMEM((1, LEAD), jnp.float32),
+            pltpu.VMEM((1, width), jnp.float32),
+            dma((2,)),
             dma((2, nr)),
             dma((2, nr)),
             dma((nr,)),

time: 54.8 us -> 49.9 us (0.911); the launches traced: 54.6 us -> 48.9 us
  Pallas kernels: 53 us -> 47.3 us
    pallas_call x1, Pallas kernels: 47.6 us -> 41.7 us  [on_device(): pl.pallas_call(functools.partial(gather_kernel, nr, nc), out_shape=(jax.S...]
where the time goes in v3:
time: 49.9 us; the launch traced here: 48.9 us
  Pallas kernels  47.3 us (95%)
  local copies, waits for them, and re-layouts  1.61 us (3%)
    pallas_call x1, Pallas kernels, on_device(): pl.pallas_call(functools.partial(gather_kernel, nr, nc), out_shape=(jax.S...  41.7 us
    pallas_call x1, Pallas kernels, on_device(): pl.pallas_call(update_kernel, grid=(width // tile,), out_shape=jax.ShapeD...  5.59 us
    unnamed x4, local copies, waits for them, and re-layouts  1.61 us

profile of v3, /device:TPU:21, one launch (start us, length us, event | category | flops | bytes accessed | tf_op | source)
XLA Modules:
  0.0 48.9 jit_solution(1221588314372622031)
XLA Ops:
  0.0 0.0 copy-start
  0.0 0.9 %copy-done = bf16[96,1024]{1,0:T(8,128)(2,1)S(1)} copy-done((bf16[96,1024]{1,0:T(8,128)(2,1)S(1)}, bf16[96,1024]{1,0:T(8,128)(2,1)}, u32[]{:S(2)}) %copy-start) | copy-done | bytes 196632
  0.9 0.0 copy-start.1
  0.9 0.7 %copy-done.1 = f32[1024]{0:T(1024)S(1)} copy-done((f32[1024]{0:T(1024)S(1)}, f32[1024]{0:T(1024)}, u32[]{:S(2)}) %copy-start.1) | copy-done | bytes 4120
  1.6 41.7 %gather_factor.1 = (bf16[384,1024]{1,0:T(8,128)(2,1)S(1)}, bf16[384,1024]{1,0:T(8,128)(2,1)S(1)}, f32[384,512]{1,0:T(8,128)S(1)}, f32[384,384]{1,0:T(8,128)S(1)}, f32[512,128]{1,0:T(8,128)S(1)}) custom-call(bf16[96,1024]{1,0:T(8,128)(2,1)S(1)} %copy-done, f32[1,1024]{1,0:T(1,128)S(1)} %bitcast.1), custom_call_target="tpu_custom_call" | custom-call | tf_op jit(solution)/shard_map/gather_factor/pallas_call | solution.py:450
  43.3 5.6 %update.1 = f32[1024,1024]{1,0:T(8,128)} custom-call(bf16[384,1024]{1,0:T(8,128)(2,1)S(1)} %get-tuple-element.10.cols_ref, bf16[384,1024]{1,0:T(8,128)(2,1)S(1)} %get-tuple-element.11.mir_ref, f32[384,512]{1,0:T(8,128)S(1)} %get-tuple-element.12.b_ref, f32[384,384]{1,0:T(8,128)S(1)} %get-tuple-element.13.w_ref, f32[512,128]{1,0:T(8,128)S(1)} %get-tuple-element.14.l_ref, ...), custom_call_target="tpu_custom_call" | custom-call | tf_op jit(solution)/shard_map/update/pallas_call | solution.py:483
Async XLA Ops:
  0.0 0.9 %copy-start = (bf16[96,1024]{1,0:T(8,128)(2,1)S(1)}, bf16[96,1024]{1,0:T(8,128)(2,1)}, u32[]{:S(2)}) copy-start(bf16[96,1024]{1,0:T(8,128)(2,1)} %a_hbm.1) | copy-start | bytes 589828
  0.9 0.7 %copy-start.1 = (f32[1024]{0:T(1024)S(1)}, f32[1024]{0:T(1024)}, u32[]{:S(2)}) copy-start(f32[1024]{0:T(1024)} %param.3) | copy-start | bytes 12292
